TPU v7x, 32 devices: a whole 2x2x4 slice. The times are simulated.
32 devices in a mesh: dp: 8 (over y, x, core), rep: 4 (over z).
Axes of the slice: x: 2, y: 2, z: 4, core: 2. Of those that a mesh axis runs over, the one named last changes fastest.
Arguments:
- images: bfloat16 [50176, 1024], P(('dp', 'rep')), may hold values from -12 to 12, as said below
- w_reduce: bfloat16 [2, 1024, 256], P(None, 'dp'), may hold values from -0.1875 to 0.1875
- w_spatial: bfloat16 [2, 2304, 256], P(None, 'dp'), may hold values from -0.125 to 0.125
- w_expand: bfloat16 [2, 256, 1024], P(None, 'dp'), may hold values from -0.375 to 0.375
- gammas: float32 [6, 1024], replicated, may hold values from 0.5 to 1.5
- betas: float32 [6, 1024], replicated, may hold values from -1.5 to 1.5
- momenta: float32 [6], replicated, may hold values from 0.2 to 0.9
- run_mean: float32 [8, 1024], P('dp'), may hold values from -3 to 3
- run_var: float32 [8, 1024], P('dp'), may hold values from 0.25 to 4
- slot_table: int32 [8], replicated, may hold values from 0 to 7, each once
Outputs:
- activations: bfloat16 [50176, 1024], P(('dp', 'rep'))
- new_mean: float32 [8, 1024], P('dp')
- new_var: float32 [8, 1024], P('dp')
Inputs may be any that keep to these rules, and one draw needn't show every extreme that they name: `slot_table`: each slot appears once. `images`: each image has its own scale and per-channel offset.
All inputs are finite; a program needn't handle non-finite values.
Results may differ from a plain program's by a relative error of at most 0.0056.
Values may be sent and summed in bfloat16 or wider, within the bound.
A program may use at most 128 MiB of HBM per device.

v0:
```python
import jax
import jax.numpy as jnp
from jax import lax
from jax.sharding import PartitionSpec as P

SIDE = 14
BLOCKS = 2


EPSILON = 0.05
RATIO_MAX = 3.0
SHIFT_MAX = 5.0


def spread(value, axis, source):
    kept = jnp.where(lax.axis_index(axis) == source, value, 0).astype(value.dtype)
    return lax.psum(kept, axis)


def conv_patches(hidden):
    count = hidden.shape[0] // (SIDE * SIDE)
    channels = hidden.shape[1]
    shaped = hidden.reshape(count, SIDE, SIDE, channels)
    padded = jnp.pad(shaped, ((0, 0), (1, 1), (1, 1), (0, 0)))
    pieces = [
        padded[:, row_off : row_off + SIDE, col_off : col_off + SIDE, :]
        for row_off in range(3)
        for col_off in range(3)
    ]
    return jnp.concatenate(pieces, axis=-1).reshape(count * SIDE * SIDE, 9 * channels)


def renorm_factors(total, squares, count, run_m, run_v, gain, offset):
    batch_mean = total / count
    batch_var = jnp.maximum(squares / count - batch_mean * batch_mean, 0.0)
    batch_sigma = jnp.sqrt(batch_var + EPSILON)
    run_sigma = jnp.sqrt(run_v + EPSILON)
    ratio = jnp.clip(batch_sigma / run_sigma, 1.0 / RATIO_MAX, RATIO_MAX)
    shift = jnp.clip((batch_mean - run_m) / run_sigma, -SHIFT_MAX, SHIFT_MAX)
    scale = gain * ratio / batch_sigma
    bias = offset + gain * (shift - ratio * batch_mean / batch_sigma)
    return (scale, bias, batch_mean, batch_var)


def whole_weight(shard):
    return lax.all_gather(shard, "dp", axis=0, tiled=True)


def channel_moments(pre):
    total = jnp.sum(pre, axis=0)
    squares = jnp.sum(pre * pre, axis=0)
    total, squares = lax.psum((total, squares), "rep")
    total, squares = lax.psum((total, squares), "dp")
    return (total, squares)


def body(
    images, w_reduce, w_spatial, w_expand, gammas, betas, momenta, run_mean, run_var, slot_table
):
    own_index = lax.axis_index("dp")
    count = 1.0 * images.shape[0] * lax.axis_size("dp") * lax.axis_size("rep")
    base_mean = run_mean[0]
    base_var = run_var[0]

    def running(layer_index):
        return (
            spread(base_mean, "dp", slot_table[layer_index]),
            spread(base_var, "dp", slot_table[layer_index]),
        )

    updates = []

    def layer_norm(pre, layer_index):
        channels = pre.shape[1]
        total, squares = channel_moments(pre)
        state_mean, state_var = running(layer_index)
        run_m = state_mean[:channels]
        run_v = state_var[:channels]
        scale, bias, batch_mean, batch_var = renorm_factors(
            total,
            squares,
            count,
            run_m,
            run_v,
            gammas[layer_index, :channels],
            betas[layer_index, :channels],
        )
        rate = momenta[layer_index]
        updates.append(
            (
                layer_index,
                channels,
                run_m + rate * (batch_mean - run_m),
                run_v + rate * (batch_var - run_v),
            )
        )
        return pre * scale + bias

    current = images
    for block_index in range(BLOCKS):
        first = 3 * block_index
        pre = jnp.dot(
            current, whole_weight(w_reduce[block_index]), preferred_element_type=jnp.float32
        )
        hidden = jax.nn.relu(layer_norm(pre, first)).astype(jnp.bfloat16)
        patches = conv_patches(hidden)
        pre = jnp.dot(
            patches, whole_weight(w_spatial[block_index]), preferred_element_type=jnp.float32
        )
        spatial = jax.nn.relu(layer_norm(pre, first + 1)).astype(jnp.bfloat16)
        pre = jnp.dot(
            spatial, whole_weight(w_expand[block_index]), preferred_element_type=jnp.float32
        )
        normed = layer_norm(pre, first + 2)
        current = jax.nn.relu(normed + current.astype(jnp.float32)).astype(jnp.bfloat16)
    out_mean = base_mean
    out_var = base_var
    for layer_index, channels, fresh_mean, fresh_var in updates:
        owned_here = slot_table[layer_index] == own_index
        full_mean = jnp.concatenate([fresh_mean, base_mean[channels:]])
        full_var = jnp.concatenate([fresh_var, base_var[channels:]])
        out_mean = jnp.where(owned_here, full_mean, out_mean)
        out_var = jnp.where(owned_here, full_var, out_var)
    return (current, out_mean[None], out_var[None])


def solution(mesh):
    in_specs = (
        P(("dp", "rep"), None),
        P(None, "dp", None),
        P(None, "dp", None),
        P(None, "dp", None),
        P(),
        P(),
        P(),
        P("dp", None),
        P("dp", None),
        P(),
    )
    out_specs = (P(("dp", "rep"), None), P("dp", None), P("dp", None))
    return jax.shard_map(body, mesh=mesh, in_specs=in_specs, out_specs=out_specs, check_vma=False)
```

profile of v0, /device:TPU:0, one launch (start us, length us, event | category | flops | bytes accessed | tf_op | source)
XLA Modules:
  0.0 399.4 jit_solution(15535920908648525998)
XLA Ops:
  24.5 13.1 %all-gather = bf16[1,1024,256]{2,1,0:T(8,128)(2,1)S(1)} all-gather(bf16[1,128,256]{2,1,0:T(8,128)(2,1)S(1)} %get-tuple-element.72), channel_id=2, replica_groups=mesh['dp'=8,'rep'=4] {'dp'}, dimensions={1}, use_global_device_ids=true | all-gather | bytes 589824 | tf_op jit(solution)/shard_map/all_gather | solution.py:46
  40.5 2.9 multiply_reduce_fusion.5
  43.5 11.8 %all-reduce.13 = (f32[256]{0:T(256)S(1)}, f32[256]{0:T(256)S(1)}) all-reduce(f32[256]{0:T(256)S(1)} %get-tuple-element.14, f32[256]{0:T(256)S(1)} %get-tuple-element.13), channel_id=1, replica_groups=mesh['dp'=8,'rep'=4] {'rep'}, use_global_device_ids=true, to_apply=%region_4.0 | all-reduce | flops 512 | bytes 4096 | tf_op jit(solution)/shard_map/psum | solution.py:52
  55.9 22.6 %all-reduce.7 = (f32[1024]{0:T(1024)S(1)}, f32[256]{0:T(256)S(1)}, f32[1024]{0:T(1024)S(1)}, f32[256]{0:T(256)S(1)}) all-reduce(f32[1024]{0:T(1024)S(1)} %get-tuple-element.110, f32[256]{0:T(256)S(1)} %get-tuple-element.49, f32[1024]{0:T(1024)S(1)} %get-tuple-element.135, ...), channel_id=1, replica_groups=mesh['dp'=8,'rep'=4] {'dp'}, use_global_device_ids=true, to_apply=%region_7.8 | all-reduce | flops 2560 | bytes 20480 | tf_op jit(solution)/shard_map/psum | solution.py:17
  81.4 6.8 %pad_slice_fusion.8 = (bf16[8,14,14,256]{3,2,1,0:T(8,128)(2,1)S(1)}, bf16[8,14,14,256]{3,2,1,0:T(8,128)(2,1)}, bf16[8,14,14,256]{3,2,1,0:T(8,128)(2,1)}, bf16[8,...) fusion(bf16[8,14,14,256]{3,2,1,0:T(8,128)(2,1)} %reshape.48), kind=kLoop, calls=%fused_computation.32 | loop fusion | bytes 7225344 | tf_op jit(solution)/shard_map/slice | solution.py:26
  90.3 2.2 constant_dynamic-update-slice_fusion.8
  112.7 9.4 %all-gather.2 = bf16[1,256,1024]{2,1,0:T(8,128)(2,1)S(1)} all-gather(bf16[1,32,1024]{2,1,0:T(8,128)(2,1)S(1)} %get-tuple-element.70), channel_id=4, replica_groups=mesh['dp'=8,'rep'=4] {'dp'}, dimensions={1}, use_global_device_ids=true | all-gather | bytes 589824 | tf_op jit(solution)/shard_map/all_gather | solution.py:46
  122.1 10.3 %all-gather.3 = bf16[1,1024,256]{2,1,0:T(8,128)(2,1)} all-gather(bf16[1,128,256]{2,1,0:T(8,128)(2,1)S(1)} %get-tuple-element.71), channel_id=5, replica_groups=mesh['dp'=8,'rep'=4] {'dp'}, dimensions={1}, use_global_device_ids=true | all-gather | bytes 589824 | tf_op jit(solution)/shard_map/all_gather | solution.py:46
  132.4 10.4 %all-gather.5 = bf16[1,256,1024]{2,1,0:T(8,128)(2,1)} all-gather(bf16[1,32,1024]{2,1,0:T(8,128)(2,1)S(1)} %get-tuple-element.69), channel_id=7, replica_groups=mesh['dp'=8,'rep'=4] {'dp'}, dimensions={1}, use_global_device_ids=true | all-gather | bytes 589824 | tf_op jit(solution)/shard_map/all_gather | solution.py:46
  144.8 2.2 constant_dynamic-update-slice_fusion.2
  149.1 5.4 %multiply_reduce_fusion.4 = (f32[256]{0:T(256)S(1)}, f32[256]{0:T(256)S(1)}, f32[1568,256]{1,0:T(8,128)S(1)}) fusion(bf16[1568,2304]{1,0:T(8,128)(2,1)} %constant_dynamic-update-slice_fusion, bf16[1,2304,256]{2,1,0:T(8,128)(2,1)} %all-gather.9.cloned.1.call-done), kind=kOutput, calls=%fused_computation.9 | convolution fusion | flops 1850891776 | bytes 10012672 | tf_op jit(solution)/shard_map/dot_general | solution.py:107
  154.5 8.4 %all-reduce.12 = (f32[256]{0:T(256)S(1)}, f32[256]{0:T(256)S(1)}) all-reduce(f32[256]{0:T(256)S(1)} %get-tuple-element.12, f32[256]{0:T(256)S(1)} %get-tuple-element.11), channel_id=1, replica_groups=mesh['dp'=8,'rep'=4] {'rep'}, use_global_device_ids=true, to_apply=%region_12.13 | all-reduce | flops 512 | bytes 4096 | tf_op jit(solution)/shard_map/psum | solution.py:52
  162.9 22.5 %all-reduce.6 = (f32[1024]{0:T(1024)S(1)}, f32[256]{0:T(256)S(1)}, f32[1024]{0:T(1024)S(1)}, f32[256]{0:T(256)S(1)}) all-reduce(f32[1024]{0:T(1024)S(1)} %copy-done.6, f32[256]{0:T(256)S(1)} %get-tuple-element.47, f32[1024]{0:T(1024)S(1)} %copy-done.7, f32[256]{0:T(256)S(1)} %get-tuple-element.48), channel_id=1, replica_groups=mesh['dp'=8,'rep'=4] {'dp'}, use_global_device_ids=true, to_apply=%region_15.16 | all-reduce | flops 2560 | bytes 20480 | tf_op jit(solution)/shard_map/psum | solution.py:17
  186.1 3.8 multiply_reduce_fusion.1
  189.9 10.5 %all-reduce.11 = (f32[1024]{0:T(1024)S(1)}, f32[1024]{0:T(1024)S(1)}) all-reduce(f32[1024]{0:T(1024)S(1)} %get-tuple-element.6, f32[1024]{0:T(1024)S(1)} %get-tuple-element.5), channel_id=1, replica_groups=mesh['dp'=8,'rep'=4] {'rep'}, use_global_device_ids=true, to_apply=%region_20.21 | all-reduce | flops 2048 | bytes 16384 | tf_op jit(solution)/shard_map/psum | solution.py:52
  200.4 22.3 %all-reduce.5 = (f32[1024]{0:T(1024)S(1)}, f32[1024]{0:T(1024)S(1)}, f32[1024]{0:T(1024)S(1)}, f32[1024]{0:T(1024)S(1)}) all-reduce(f32[1024]{0:T(1024)S(1)} %copy-done.11, f32[1024]{0:T(1024)S(1)} %get-tuple-element.45, f32[1024]{0:T(1024)S(1)} %copy-done.10, f32[1024]{0:T(1024)S(1)} %get-tuple-element.46), channel_id=1, replica_groups=mesh['dp'=8,'rep'=4] {'dp'}, use_global_device_ids=true, to_apply=%region_22.23 | all-reduce | flops 4096 | bytes 32768 | tf_op jit(solution)/shard_map/psum | solution.py:17
  222.8 5.2 %maximum_convert_fusion.1 = bf16[1568,1024]{1,0:T(8,128)(2,1)S(1)} fusion(bf16[1568,1024]{1,0:T(8,128)(2,1)} %param.10, f32[1568,1024]{1,0:T(8,128)} %get-tuple-element.131, f32[1024]{0:T(1024)S(1)} %get-tuple-element.88, f32[1024]{0:T(1024)S(1)} %get-tuple-element.87), kind=kLoop, calls=%fused_computation.2 | loop fusion | flops 9633792 | bytes 12853248 | tf_op jit(solution)/shard_map/convert_element_type | solution.py:115
  230.1 8.3 %all-reduce.10 = (f32[256]{0:T(256)S(1)}, f32[256]{0:T(256)S(1)}) all-reduce(f32[256]{0:T(256)S(1)} %get-tuple-element.10, f32[256]{0:T(256)S(1)} %get-tuple-element.9), channel_id=1, replica_groups=mesh['dp'=8,'rep'=4] {'rep'}, use_global_device_ids=true, to_apply=%region_28.29 | all-reduce | flops 512 | bytes 4096 | tf_op jit(solution)/shard_map/psum | solution.py:52
  238.5 22.3 %all-reduce.4 = (f32[1024]{0:T(1024)S(1)}, f32[256]{0:T(256)S(1)}, f32[1024]{0:T(1024)S(1)}, f32[256]{0:T(256)S(1)}) all-reduce(f32[1024]{0:T(1024)S(1)} %get-tuple-element.107, f32[256]{0:T(256)S(1)} %get-tuple-element.43, f32[1024]{0:T(1024)S(1)} %get-tuple-element.138, ...), channel_id=1, replica_groups=mesh['dp'=8,'rep'=4] {'dp'}, use_global_device_ids=true, to_apply=%region_31.32 | all-reduce | flops 2560 | bytes 20480 | tf_op jit(solution)/shard_map/psum | solution.py:17
  261.4 2.5 maximum_convert_fusion.3
  266.1 7.0 %pad_slice_fusion = (bf16[8,14,14,256]{3,2,1,0:T(8,128)(2,1)}, bf16[8,14,14,256]{3,2,1,0:T(8,128)(2,1)}, bf16[8,14,14,256]{3,2,1,0:T(8,128)(2,1)}, bf16[8,14,14,...) fusion(bf16[8,14,14,256]{3,2,1,0:T(8,128)(2,1)} %reshape.49), kind=kLoop, calls=%fused_computation.24 | loop fusion | bytes 7225344 | tf_op jit(solution)/shard_map/slice | solution.py:26
  275.2 2.2 constant_dynamic-update-slice_fusion.17
  283.8 2.2 concatenate.76
  294.5 2.3 constant_dynamic-update-slice_fusion.15
  298.9 2.6 constant_dynamic-update-slice_fusion.13
  306.7 6.5 %multiply_reduce_fusion.2 = (f32[256]{0:T(256)S(1)}, f32[256]{0:T(256)S(1)}, f32[1568,256]{1,0:T(8,128)}) fusion(bf16[1568,2304]{1,0:T(8,128)(2,1)} %constant_dynamic-update-slice_fusion.9, bf16[1,2304,256]{2,1,0:T(8,128)(2,1)} %all-gather.11.cloned.1.call-done), kind=kOutput, calls=%fused_computation.5 | convolution fusion | flops 1850891776 | bytes 10012672 | tf_op jit(solution)/shard_map/dot_general | solution.py:107
  313.3 10.3 %all-reduce.9 = (f32[256]{0:T(256)S(1)}, f32[256]{0:T(256)S(1)}) all-reduce(f32[256]{0:T(256)S(1)} %get-tuple-element.8, f32[256]{0:T(256)S(1)} %get-tuple-element.7), channel_id=1, replica_groups=mesh['dp'=8,'rep'=4] {'rep'}, use_global_device_ids=true, to_apply=%region_36.37 | all-reduce | flops 512 | bytes 4096 | tf_op jit(solution)/shard_map/psum | solution.py:52
  323.6 22.5 %all-reduce.3 = (f32[1024]{0:T(1024)S(1)}, f32[256]{0:T(256)S(1)}, f32[1024]{0:T(1024)S(1)}, f32[256]{0:T(256)S(1)}) all-reduce(f32[1024]{0:T(1024)S(1)} %get-tuple-element.106, f32[256]{0:T(256)S(1)} %get-tuple-element.41, f32[1024]{0:T(1024)S(1)} %get-tuple-element.139, ...), channel_id=1, replica_groups=mesh['dp'=8,'rep'=4] {'dp'}, use_global_device_ids=true, to_apply=%region_39.40 | all-reduce | flops 2560 | bytes 20480 | tf_op jit(solution)/shard_map/psum | solution.py:17
  346.8 5.3 %multiply_reduce_fusion = (f32[1024]{0:T(1024)S(1)}, f32[1024]{0:T(1024)S(1)}, f32[1568,1024]{1,0:T(8,128)}) fusion(bf16[1,256,1024]{2,1,0:T(8,128)(2,1)} %all-gather.5, f32[1568,256]{1,0:T(8,128)} %get-tuple-element.133, f32[256]{0:T(256)S(1)} %get-tuple-element.90, f32[256]{0:T(256)S(1)} %get-tuple-element.89), kind=kOutput, calls=%fused_computation.1 | convolution fusion | flops 828504064 | bytes 8562688 | tf_op jit(solution)/shard_map/dot_general | solution.py:111
  352.1 8.5 %all-reduce.8 = (f32[1024]{0:T(1024)S(1)}, f32[1024]{0:T(1024)S(1)}) all-reduce(f32[1024]{0:T(1024)S(1)} %get-tuple-element.4, f32[1024]{0:T(1024)S(1)} %get-tuple-element.3), channel_id=1, replica_groups=mesh['dp'=8,'rep'=4] {'rep'}, use_global_device_ids=true, to_apply=%region_44.45 | all-reduce | flops 2048 | bytes 16384 | tf_op jit(solution)/shard_map/psum | solution.py:52
  360.6 22.3 %all-reduce.2 = (f32[1024]{0:T(1024)S(1)}, f32[1024]{0:T(1024)S(1)}, f32[1024]{0:T(1024)S(1)}, f32[1024]{0:T(1024)S(1)}) all-reduce(f32[1024]{0:T(1024)S(1)} %copy-done.9, f32[1024]{0:T(1024)S(1)} %get-tuple-element.39, f32[1024]{0:T(1024)S(1)} %copy-done.8, f32[1024]{0:T(1024)S(1)} %get-tuple-element.40), channel_id=1, replica_groups=mesh['dp'=8,'rep'=4] {'dp'}, use_global_device_ids=true, to_apply=%region_46.47 | all-reduce | flops 4096 | bytes 32768 | tf_op jit(solution)/shard_map/psum | solution.py:17
  383.0 5.8 %maximum_convert_fusion = bf16[1568,1024]{1,0:T(8,128)(2,1)} fusion(bf16[1568,1024]{1,0:T(8,128)(2,1)S(1)} %maximum_convert_fusion.1, f32[1568,1024]{1,0:T(8,128)} %get-tuple-element.134, f32[1024]{0:T(1024)S(1)} %get-tuple-element.86, f32[1024]{0:T(1024)S(1)} %get-tuple-element.85), kind=kLoop, calls=%fused_computation | loop fusion | flops 9633792 | bytes 12853248 | tf_op jit(solution)/shard_map/convert_element_type | solution.py:115
  (102 shorter events, 76.9 us)
Async XLA Ops:
  7.2 48.1 %copy-start.5 = (f32[1,1024]{1,0:T(1,128)S(1)}, f32[1,1024]{1,0:T(1,128)}, u32[]{:S(2)}) copy-start(f32[1,1024]{1,0:T(1,128)} %param.18) | copy-start | bytes 12292
  7.2 48.1 %copy-start.4 = (f32[1,1024]{1,0:T(1,128)S(1)}, f32[1,1024]{1,0:T(1,128)}, u32[]{:S(2)}) copy-start(f32[1,1024]{1,0:T(1,128)} %param.17) | copy-start | bytes 12292
  7.2 141.9 %all-gather.9.cloned.1.call-start = ((), (), s32[]{:S(2)}) async-start(), calls=%async_computation | async-start | bytes 1327104 | tf_op jit(solution)/shard_map/all_gather | solution.py:46
  9.0 297.7 %all-gather.11.cloned.1.call-start = ((), (), s32[]{:S(2)}) async-start(), calls=%async_computation.1 | async-start | bytes 1327104 | tf_op jit(solution)/shard_map/all_gather | solution.py:46
  79.7 0.6 copy-start.12
  79.7 0.6 copy-start.13
  149.1 13.8 %copy-start.6 = (f32[1024]{0:T(1024)S(1)}, f32[1024]{0:T(1024)}, u32[]{:S(2)}) copy-start(f32[1024]{0:T(1024)} %get-tuple-element.109) | copy-start | bytes 12292
  149.1 13.8 %copy-start.7 = (f32[1024]{0:T(1024)S(1)}, f32[1024]{0:T(1024)}, u32[]{:S(2)}) copy-start(f32[1024]{0:T(1024)} %get-tuple-element.136) | copy-start | bytes 12292
  149.1 36.3 %copy-start.20 = (f32[1,256]{1,0:T(1,128)S(1)}, f32[1,256]{1,0:T(1,128)}, u32[]{:S(2)}) copy-start(f32[1,256]{1,0:T(1,128)} %get-tuple-element.79) | copy-start | bytes 3076
  149.1 36.3 %copy-start.21 = (f32[1,256]{1,0:T(1,128)S(1)}, f32[1,256]{1,0:T(1,128)}, u32[]{:S(2)}) copy-start(f32[1,256]{1,0:T(1,128)} %get-tuple-element.83) | copy-start | bytes 3076
  186.1 14.3 %copy-start.10 = (f32[1024]{0:T(1024)S(1)}, f32[1024]{0:T(1024)}, u32[]{:S(2)}) copy-start(f32[1024]{0:T(1024)} %get-tuple-element.108) | copy-start | bytes 12292
  186.1 14.3 %copy-start.11 = (f32[1024]{0:T(1024)S(1)}, f32[1024]{0:T(1024)}, u32[]{:S(2)}) copy-start(f32[1024]{0:T(1024)} %get-tuple-element.137) | copy-start | bytes 12292
  222.8 5.2 %copy-start.3 = (bf16[1,1024,256]{2,1,0:T(8,128)(2,1)S(1)}, bf16[1,1024,256]{2,1,0:T(8,128)(2,1)}, u32[]{:S(2)}) copy-start(bf16[1,1024,256]{2,1,0:T(8,128)(2,1)} %all-gather.3) | copy-start | bytes 1572868
  228.0 32.8 %copy-start.18 = (f32[1,256]{1,0:T(1,128)S(1)}, f32[1,256]{1,0:T(1,128)}, u32[]{:S(2)}) copy-start(f32[1,256]{1,0:T(1,128)} %get-tuple-element.78) | copy-start | bytes 3076
  228.0 32.8 %copy-start.19 = (f32[1,256]{1,0:T(1,128)S(1)}, f32[1,256]{1,0:T(1,128)}, u32[]{:S(2)}) copy-start(f32[1,256]{1,0:T(1,128)} %get-tuple-element.82) | copy-start | bytes 3076
  294.5 9.1 %copy-start.2 = (bf16[1568,256]{1,0:T(8,128)(2,1)S(1)}, bf16[1568,256]{1,0:T(8,128)(2,1)}, u32[]{:S(2)}) copy-start(bf16[1568,256]{1,0:T(8,128)(2,1)} %concatenate.78) | copy-start | bytes 2408452
  294.5 10.2 %copy-start = (bf16[1568,256]{1,0:T(8,128)(2,1)S(1)}, bf16[1568,256]{1,0:T(8,128)(2,1)}, u32[]{:S(2)}) copy-start(bf16[1568,256]{1,0:T(8,128)(2,1)} %concatenate.79) | copy-start | bytes 2408452
  294.5 11.2 %copy-start.1 = (bf16[1568,256]{1,0:T(8,128)(2,1)S(1)}, bf16[1568,256]{1,0:T(8,128)(2,1)}, u32[]{:S(2)}) copy-start(bf16[1568,256]{1,0:T(8,128)(2,1)} %concatenate.80) | copy-start | bytes 2408452
  306.7 39.4 %copy-start.16 = (f32[1,256]{1,0:T(1,128)S(1)}, f32[1,256]{1,0:T(1,128)}, u32[]{:S(2)}) copy-start(f32[1,256]{1,0:T(1,128)} %get-tuple-element.77) | copy-start | bytes 3076
  306.7 39.4 %copy-start.17 = (f32[1,256]{1,0:T(1,128)S(1)}, f32[1,256]{1,0:T(1,128)}, u32[]{:S(2)}) copy-start(f32[1,256]{1,0:T(1,128)} %get-tuple-element.81) | copy-start | bytes 3076
  346.7 13.8 %copy-start.8 = (f32[1024]{0:T(1024)S(1)}, f32[1024]{0:T(1024)}, u32[]{:S(2)}) copy-start(f32[1024]{0:T(1024)} %get-tuple-element.105) | copy-start | bytes 12292
  346.8 13.8 %copy-start.9 = (f32[1024]{0:T(1024)S(1)}, f32[1024]{0:T(1024)}, u32[]{:S(2)}) copy-start(f32[1024]{0:T(1024)} %get-tuple-element.140) | copy-start | bytes 12292
  383.0 5.8 %copy-start.15 = (f32[256]{0:T(256)S(1)}, f32[256]{0:T(256)}, u32[]{:S(2)}) copy-start(f32[256]{0:T(256)} %get-tuple-element.97) | copy-start | bytes 3076
  383.0 7.7 %copy-start.14 = (f32[256]{0:T(256)S(1)}, f32[256]{0:T(256)}, u32[]{:S(2)}) copy-start(f32[256]{0:T(256)} %get-tuple-element.104) | copy-start | bytes 3076
Sparse Core Ops, SparseCore 0:
  9.9 28.2 all-gather.8
  40.0 24.0 all-gather.10
where the time goes:
time: 401 us; the launch traced here: 399 us
  blocking collectives  236 us (59%)
  local copies, waits for them, and re-layouts  89.3 us (22%)
  matrix products  26.1 us (7%)
  other arithmetic  25.6 us (6%)
  between operations  22 us (5%)
    psum x6, blocking collectives, spread(): return lax.psum(kept, axis)  135 us
    psum x6, blocking collectives, channel_moments(): total, squares = lax.psum((total, squares), 'rep')  57.8 us
    all_gather x4, blocking collectives, whole_weight(): return lax.all_gather(shard, 'dp', axis=0, tiled=True)  43.1 us
    concatenate x18, local copies, waits for them, and re-layouts, conv_patches(): jnp.concatenate(pieces, axis=-1).reshape(count * SIDE * SIDE, 9 * channels)  32.2 us
    unnamed x58, local copies, waits for them, and re-layouts  27.4 us
    slice x2, local copies, waits for them, and re-layouts, conv_patches(): padded[:, row_off:row_off + SIDE, col_off:col_off + SIDE, :]  13.8 us
    dot_general x2, matrix products, body(): jnp.dot(patches, whole_weight(w_spatial[block_index]), preferred_element_...  11.9 us
    convert_element_type x2, other arithmetic, body(): jax.nn.relu(normed + current.astype(jnp.float32)).astype(jnp.bfloat16)  11 us
  transfers between devices with their start and end apart: 2, of which 0 were waited for; matrix products, arithmetic and copies ran while one was open for 29% of the time, Pallas kernels for 0%

commit v1 on v0

v1 whole, which is shorter than its diff:
```python
import functools
import jax
import jax.numpy as jnp
from jax import lax
from jax.experimental import pallas as pl
from jax.experimental.pallas import tpu as pltpu
from jax.sharding import PartitionSpec as P

SIDE = 14
WIDE = 16
BLOCKS = 2
LAYERS = 6
MARGIN = 8
EPSILON = 0.05
RATIO_MAX = 3.0
SHIFT_MAX = 5.0
MESH = pl.DeviceIdType.MESH


def renorm_factors(total, squares, count, run_m, run_v, gain, offset):
    batch_mean = total / count
    batch_var = jnp.maximum(squares / count - batch_mean * batch_mean, 0.0)
    batch_sigma = jnp.sqrt(batch_var + EPSILON)
    run_sigma = jnp.sqrt(run_v + EPSILON)
    ratio = jnp.clip(batch_sigma / run_sigma, 1.0 / RATIO_MAX, RATIO_MAX)
    shift = jnp.clip((batch_mean - run_m) / run_sigma, -SHIFT_MAX, SHIFT_MAX)
    scale = gain * ratio / batch_sigma
    bias = offset + gain * (shift - ratio * batch_mean / batch_sigma)
    return (scale, bias, batch_mean, batch_var)


def kernel(
    dp, rep, gather, slot_ref, rate_ref, images, w_reduce, w_spatial, w_expand, gammas, betas,
    run_mean, run_var, out, new_mean, new_var,
    cur, pre_n, pre_w, hid, spa, w_r, w_s, w_e, rows_all, stat_d, stat_r,
    in_sem, out_sem, load_sem, w_send, w_recv, rows_send, rows_recv, d_send, d_recv, r_send, r_recv,
):
    pix, wide_c = cur.shape
    thin_c = pre_n.shape[2]
    imgs = pix // (SIDE * SIDE)
    half = imgs // 2
    count = 1.0 * pix * dp * rep
    me = lax.axis_index("dp")
    mine = lax.axis_index("rep")
    sibling = me + 1 - 2 * lax.rem(me, 2)
    pairs = dp // 2

    full = {"r": w_r, "s": w_s, "e": w_e}
    given = {"r": w_reduce, "s": w_spatial, "e": w_expand}
    parts = [(b, kind) for b in range(BLOCKS) for kind in "rse"]

    def slot_of(part, owner):
        b, kind = parts[part]
        depth = given[kind].shape[1]
        return full[kind].at[b, pl.ds(pl.multiple_of(owner * depth, depth), depth), :]

    loads = []
    for part, (b, kind) in enumerate(parts):
        target = slot_of(part, me) if gather else full[kind].at[b]
        loads.append(pltpu.make_async_copy(given[kind].at[b], target, load_sem.at[part]))
    row_loads = [
        pltpu.make_async_copy(run_mean, rows_all.at[me, pl.ds(0, 1)], load_sem.at[len(parts)]),
        pltpu.make_async_copy(run_var, rows_all.at[me, pl.ds(1, 1)], load_sem.at[len(parts) + 1]),
    ]
    loads[0].start()
    for copy in row_loads:
        copy.start()
    for copy in loads[1:]:
        copy.start()
    step = pix // 7
    image_loads = [
        pltpu.make_async_copy(
            images.at[pl.ds(i * step, step)], cur.at[pl.ds(i * step, step)], in_sem.at[i]
        )
        for i in range(7)
    ]
    for copy in image_loads:
        copy.start()

    barrier = pltpu.get_barrier_semaphore()
    for k in range(1, dp):
        pl.semaphore_signal(
            barrier, inc=1, device_id={"dp": lax.rem(me + k, dp)}, device_id_type=MESH
        )
    for k in range(1, rep):
        pl.semaphore_signal(
            barrier, inc=1, device_id={"rep": lax.rem(mine + k, rep)}, device_id_type=MESH
        )
    hid[:, 0:1] = jnp.zeros((imgs, 1, WIDE, hid.shape[3]), hid.dtype)
    hid[:, SIDE + 1 : SIDE + 2] = jnp.zeros((imgs, 1, WIDE, hid.shape[3]), hid.dtype)
    duo = 2 * SIDE * SIDE
    pre_n[:, 0:MARGIN] = jnp.zeros((imgs // 2, MARGIN, thin_c), jnp.float32)
    pre_n[:, MARGIN + duo :] = jnp.zeros((imgs // 2, WIDE, thin_c), jnp.float32)
    pl.semaphore_wait(barrier, dp + rep - 2)

    pending = []

    def remote(src, dst, send, recv, where):
        return pltpu.make_async_remote_copy(
            src_ref=src, dst_ref=dst, send_sem=send, recv_sem=recv,
            device_id=where, device_id_type=MESH,
        )

    def w_copy(part, owner, k, where):
        ref = slot_of(part, owner)
        return remote(ref, ref, w_send.at[part, k], w_recv.at[part, k], {"dp": where})

    def w_begin(part):
        loads[part].wait()
        if not gather:
            return
        for k in range(1, pairs):
            copy = w_copy(part, me, k, lax.rem(me + 2 * k, dp))
            copy.start()
            pending.append(copy)
        copy = w_copy(part, me, 0, sibling)
        copy.start()
        pending.append(copy)

    def w_forward(part):
        if not gather:
            return
        for k in range(1, pairs):
            owner = lax.rem(me + dp - 2 * k, dp)
            w_copy(part, owner, k, sibling).wait_recv()
            copy = w_copy(part, owner, pairs + k, sibling)
            copy.start()
            pending.append(copy)

    def w_finish(part):
        if not gather:
            return
        w_copy(part, sibling, 0, sibling).wait_recv()
        for k in range(1, pairs):
            owner = lax.rem(sibling + dp - 2 * k, dp)
            w_copy(part, owner, pairs + k, sibling).wait_recv()

    w_begin(0)
    for copy in row_loads:
        copy.wait()
    row_copies = []
    for k in range(1, dp):
        ref = rows_all.at[me]
        copy = remote(
            ref, ref, rows_send.at[k], rows_recv.at[k], {"dp": lax.rem(me + k, dp)}
        )
        copy.start()
        pending.append(copy)
        row_copies.append(copy)
    w_begin(1)
    for copy in image_loads:
        copy.wait()
    w_forward(0)
    w_finish(0)

    def moments_begin(layer, total, squares):
        n = total.shape[1]
        stat_d[layer, me, 0:1, 0:n] = total
        stat_d[layer, me, 1:2, 0:n] = squares
        ref = stat_d.at[layer, me, :, pl.ds(0, n)]
        for k in range(1, dp):
            copy = remote(
                ref, ref, d_send.at[layer, k], d_recv.at[layer, k],
                {"dp": lax.rem(me + k, dp)},
            )
            copy.start()
            pending.append(copy)

    def moments_end(layer, n):
        for k in range(1, dp):
            ref = stat_d.at[layer, lax.rem(me + dp - k, dp), :, pl.ds(0, n)]
            remote(
                ref, ref, d_send.at[layer, k], d_recv.at[layer, k], {"dp": sibling}
            ).wait_recv()
        stat_r[layer, mine, :, 0:n] = jnp.sum(stat_d[layer, :, :, 0:n], axis=0)
        ref = stat_r.at[layer, mine, :, pl.ds(0, n)]
        for k in range(1, rep):
            copy = remote(
                ref, ref, r_send.at[layer, k], r_recv.at[layer, k],
                {"rep": lax.rem(mine + k, rep)},
            )
            copy.start()
            pending.append(copy)
        for k in range(1, rep):
            ref = stat_r.at[layer, lax.rem(mine + rep - k, rep), :, pl.ds(0, n)]
            remote(
                ref, ref, r_send.at[layer, k], r_recv.at[layer, k],
                {"rep": lax.rem(mine + k, rep)},
            ).wait_recv()
        both = jnp.sum(stat_r[layer, :, :, 0:n], axis=0)
        total, squares = both[0:1], both[1:2]
        rows = rows_all[slot_ref[layer]]
        run_m, run_v = rows[0:1, 0:n], rows[1:2, 0:n]
        scale, bias, batch_mean, batch_var = renorm_factors(
            total, squares, count, run_m, run_v,
            gammas[layer : layer + 1, 0:n], betas[layer : layer + 1, 0:n],
        )
        rate = rate_ref[layer]
        owned = slot_ref[layer] == me
        new_mean[:, 0:n] = jnp.where(owned, run_m + rate * (batch_mean - run_m), new_mean[:, 0:n])
        new_var[:, 0:n] = jnp.where(owned, run_v + rate * (batch_var - run_v), new_var[:, 0:n])
        return scale, bias

    def sums(value):
        return (
            jnp.sum(value, axis=0, keepdims=True),
            jnp.sum(value * value, axis=0, keepdims=True),
        )

    def add(left, right):
        return right if left is None else (left[0] + right[0], left[1] + right[1])

    new_mean[...] = run_mean_v(rows_all, me, 0)
    new_var[...] = run_mean_v(rows_all, me, 1)

    chunk = half * SIDE * SIDE

    def narrow(c):
        value = pre_n[c * (half // 2) : (c + 1) * (half // 2), MARGIN : MARGIN + duo]
        return value.reshape(chunk, thin_c)

    scale3 = bias3 = None
    for b in range(BLOCKS):
        acc = None
        for c in range(2):
            at = pl.ds(c * chunk, chunk)
            if b > 0:
                cur[at] = jax.nn.relu(
                    pre_w[at] * scale3 + bias3 + cur[at].astype(jnp.float32)
                ).astype(cur.dtype)
            pre = jnp.dot(cur[at], w_r[b], preferred_element_type=jnp.float32)
            for i in range(half // 2):
                pre_n[c * (half // 2) + i, MARGIN : MARGIN + duo] = pre[i * duo : (i + 1) * duo]
            acc = add(acc, sums(pre))
        moments_begin(3 * b, *acc)
        if b == 0:
            w_begin(2)
            w_begin(3)
            w_forward(1)
            for k, copy in enumerate(row_copies):
                copy.wait_recv()
        else:
            w_forward(5)
        scale, bias = moments_end(3 * b, thin_c)
        w_finish(3 * b + 1)

        column = lax.broadcasted_iota(jnp.int32, (WIDE, thin_c), 0)

        def fill(pair, carry):
            for i in range(2):
                for r in range(SIDE):
                    for dx in range(3):
                        start = MARGIN + i * SIDE * SIDE + r * SIDE + dx - 1
                        value = pre_n[pair, start : start + WIDE]
                        value = jax.nn.relu(value * scale + bias)
                        if dx == 0:
                            value = jnp.where(column == 0, 0.0, value)
                        if dx == 2:
                            value = jnp.where(column == SIDE - 1, 0.0, value)
                        hid[pair * 2 + i, r + 1, :, dx * thin_c : (dx + 1) * thin_c] = (
                            value.astype(hid.dtype)
                        )
            return carry

        lax.fori_loop(0, imgs // 2, fill, 0)
        acc = None
        for c in range(2):
            pre = None
            for dy in range(3):
                lhs = hid[c * half : (c + 1) * half, dy : dy + SIDE]
                lhs = lhs.reshape(half * SIDE * WIDE, 3 * thin_c)
                term = jnp.dot(
                    lhs, w_s[b, dy * 3 * thin_c : (dy + 1) * 3 * thin_c],
                    preferred_element_type=jnp.float32,
                )
                pre = term if pre is None else pre + term
            for r in range(half * SIDE):
                pair, start = divmod(c * chunk + r * SIDE, duo)
                pre_n[pair, MARGIN + start : MARGIN + start + SIDE] = pre[
                    r * WIDE : r * WIDE + SIDE
                ]
            acc = add(acc, sums(narrow(c)))
        moments_begin(3 * b + 1, *acc)
        if b == 0:
            w_begin(4)
            w_forward(2)
            w_forward(3)
        scale, bias = moments_end(3 * b + 1, thin_c)
        w_finish(3 * b + 2)

        acc = None
        for c in range(2):
            at = pl.ds(c * chunk, chunk)
            spa[at] = jax.nn.relu(
                narrow(c) * scale + bias
            ).astype(spa.dtype)
            pre = jnp.dot(spa[at], w_e[b], preferred_element_type=jnp.float32)
            pre_w[at] = pre
            acc = add(acc, sums(pre))
        moments_begin(3 * b + 2, *acc)
        if b == 0:
            w_begin(5)
            w_forward(4)
        scale3, bias3 = moments_end(3 * b + 2, wide_c)
        if b == 0:
            w_finish(3)

    stores = []
    for i in range(7):
        at = pl.ds(i * step, step)
        cur[at] = jax.nn.relu(
            pre_w[at] * scale3 + bias3 + cur[at].astype(jnp.float32)
        ).astype(cur.dtype)
        copy = pltpu.make_async_copy(cur.at[at], out.at[at], out_sem.at[i])
        copy.start()
        stores.append(copy)
    for copy in pending:
        copy.wait_send()
    for copy in stores:
        copy.wait()


def run_mean_v(rows_all, me, which):
    return rows_all[me, which : which + 1]


def body(
    images, w_reduce, w_spatial, w_expand, gammas, betas, momenta, run_mean, run_var, slot_table
):
    dp, rep = lax.axis_size("dp"), lax.axis_size("rep")
    pix, wide_c = images.shape
    thin_c = w_reduce.shape[2]
    imgs = pix // (SIDE * SIDE)
    gather = all(w.shape[1] % 16 == 0 for w in (w_reduce, w_spatial, w_expand))
    if not gather:
        w_reduce, w_spatial, w_expand = [
            lax.all_gather(w, "dp", axis=1, tiled=True) for w in (w_reduce, w_spatial, w_expand)
        ]
    anywhere = pl.BlockSpec(memory_space=pl.ANY)
    vmem = pl.BlockSpec(memory_space=pltpu.VMEM)
    smem = pl.BlockSpec(memory_space=pltpu.SMEM)
    bf16, f32 = jnp.bfloat16, jnp.float32
    dma = pltpu.SemaphoreType.DMA
    parts = 3 * BLOCKS
    return pl.pallas_call(
        functools.partial(kernel, dp, rep, gather),
        name="recalibrate",
        out_shape=(
            jax.ShapeDtypeStruct(images.shape, bf16),
            jax.ShapeDtypeStruct(run_mean.shape, f32),
            jax.ShapeDtypeStruct(run_var.shape, f32),
        ),
        in_specs=[smem, smem] + [anywhere] * 4 + [vmem, vmem, anywhere, anywhere],
        out_specs=(anywhere, vmem, vmem),
        scratch_shapes=[
            pltpu.VMEM((pix, wide_c), bf16),
            pltpu.VMEM((imgs // 2, MARGIN + 2 * SIDE * SIDE + WIDE, thin_c), f32),
            pltpu.VMEM((pix, wide_c), f32),
            pltpu.VMEM((imgs, SIDE + 2, WIDE, 3 * thin_c), bf16),
            pltpu.VMEM((pix, thin_c), bf16),
            pltpu.VMEM((BLOCKS, wide_c, thin_c), bf16),
            pltpu.VMEM((BLOCKS, 9 * thin_c, thin_c), bf16),
            pltpu.VMEM((BLOCKS, thin_c, wide_c), bf16),
            pltpu.VMEM((dp, 2, wide_c), f32),
            pltpu.VMEM((LAYERS, dp, 2, wide_c), f32),
            pltpu.VMEM((LAYERS, rep, 2, wide_c), f32),
            dma((7,)),
            dma((7,)),
            dma((parts + 2,)),
            dma((parts, dp)),
            dma((parts, dp)),
            dma((dp,)),
            dma((dp,)),
            dma((LAYERS, dp)),
            dma((LAYERS, dp)),
            dma((LAYERS, rep)),
            dma((LAYERS, rep)),
        ],
        compiler_params=pltpu.CompilerParams(
            collective_id=0, has_side_effects=True, vmem_limit_bytes=60 * 1024 * 1024
        ),
    )(slot_table, momenta, images, w_reduce, w_spatial, w_expand, gammas, betas, run_mean, run_var)


def solution(mesh):
    in_specs = (
        P(("dp", "rep"), None),
        P(None, "dp", None),
        P(None, "dp", None),
        P(None, "dp", None),
        P(),
        P(),
        P(),
        P("dp", None),
        P("dp", None),
        P(),
    )
    out_specs = (P(("dp", "rep"), None), P("dp", None), P("dp", None))
    return jax.shard_map(body, mesh=mesh, in_specs=in_specs, out_specs=out_specs, check_vma=False)
```

time: 401 us -> 78.9 us (0.20)
  blocking collectives: 236 us -> 0 us
  local copies, waits for them, and re-layouts: 89.3 us -> 5.1 us
  Pallas kernels: 0 us -> 72.9 us
  matrix products: 26.1 us -> 0 us
  other arithmetic: 25.6 us -> 0 us
  between operations: 22 us -> 0.66 us
    psum x12 -> x0, blocking collectives: 192 us -> none  [the longest x6 135 us: spread(): return lax.psum(kept, axis)]
    pallas_call x0 -> x1, Pallas kernels: none -> 72.9 us  [body(): pl.pallas_call(functools.partial(kernel, dp, rep, gather), name='recalibr...]
    all_gather x4 -> x0, blocking collectives: 43.1 us -> none  [whole_weight(): return lax.all_gather(shard, 'dp', axis=0, tiled=True)]
    concatenate x18 -> x0, local copies, waits for them, and re-layouts: 32.2 us -> none  [conv_patches(): jnp.concatenate(pieces, axis=-1).reshape(count * SIDE * SIDE, 9 * channels)]
    slice x13 -> x0, local copies, waits for them, and re-layouts: 26.4 us -> none  [the longest x2 13.8 us: conv_patches(): padded[:, row_off:row_off + SIDE, col_off:col_off + SIDE, :]]
    dot_general x6 -> x0, matrix products: 26.1 us -> none  [the longest x2 11.9 us: body(): jnp.dot(patches, whole_weight(w_spatial[block_index]), preferred_element_...]
    unnamed x58 -> x7, local copies, waits for them, and re-layouts: 27.4 us -> 5.1 us
    convert_element_type x4 -> x0, other arithmetic: 13.7 us -> none  [the longest x2 11 us: body(): jax.nn.relu(normed + current.astype(jnp.float32)).astype(jnp.bfloat16)]
  transfers between devices with their start and end apart: 2 -> 0, of which waited for: 0 -> 0; matrix products, arithmetic and copies ran while one was open for 29% -> 0% of each run, Pallas kernels for 0% -> 0%
where the time goes in v1:
time: 78.9 us; the launch traced here: 78.7 us
  Pallas kernels  72.9 us (92%)
  local copies, waits for them, and re-layouts  5.1 us (6%)
    pallas_call x1, Pallas kernels, body(): pl.pallas_call(functools.partial(kernel, dp, rep, gather), name='recalibr...  72.9 us
    unnamed x7, local copies, waits for them, and re-layouts  5.1 us

profile of v1, /device:TPU:0, one launch (start us, length us, event | category | flops | bytes accessed | tf_op | source)
XLA Modules:
  0.0 78.7 jit_solution(11865596795218060785)
XLA Ops:
  0.6 72.9 %recalibrate.1 = (bf16[1568,1024]{1,0:T(8,128)(2,1)}, f32[1,1024]{1,0:T(1,128)}, f32[1,1024]{1,0:T(1,128)}) custom-call(s32[8]{0:T(128)} %slot_ref.1, f32[6]{0:T(128)} %rate_ref.1, bf16[1568,1024]{1,0:T(8,128)(2,1)} %images.1, bf16[2,128,256]{2,1,0:T(8,128)(2,1)} %w_reduce.1, bf16[2,288,256]{2,1,0:T(8,128)(2,1)} %w_spatial.1, bf16[2,32,1024]{2,1,0:T(8,128)(2,1)} %w_expand.1, ...), custom_call_target="tpu_custom_call" | custom-call | tf_op jit(solution)/shard_map/recalibrate/pallas_call | solution.py:345
  73.6 0.0 copy-start.1
  73.6 0.0 copy-start
  73.6 3.9 %copy.16 = bf16[1568,1024]{1,0:T(8,128)(2,1)} copy(bf16[1568,1024]{1,0:T(8,128)(2,1)} %get-tuple-element.6) | data formatting | bytes 6422528
  77.5 0.0 copy-done.1
  77.5 0.6 copy.17
  78.1 0.0 copy-done
  78.1 0.6 copy.18
Async XLA Ops:
  73.6 3.9 %copy-start.1 = (f32[1,1024]{1,0:T(1,128)S(1)}, f32[1,1024]{1,0:T(1,128)}, u32[]{:S(2)}) copy-start(f32[1,1024]{1,0:T(1,128)} %get-tuple-element.7) | copy-start | bytes 12292
  73.6 4.5 %copy-start = (f32[1,1024]{1,0:T(1,128)S(1)}, f32[1,1024]{1,0:T(1,128)}, u32[]{:S(2)}) copy-start(f32[1,1024]{1,0:T(1,128)} %get-tuple-element.8) | copy-start | bytes 12292

commit v2 on v1

--- a/solution.py
+++ b/solution.py
@@ -11,6 +11,7 @@
 BLOCKS = 2
 LAYERS = 6
 MARGIN = 8
+LANES = 128
 EPSILON = 0.05
 RATIO_MAX = 3.0
 SHIFT_MAX = 5.0
@@ -30,13 +31,14 @@
 
 
 def kernel(
-    dp, rep, gather, slot_ref, rate_ref, images, w_reduce, w_spatial, w_expand, gammas, betas,
-    run_mean, run_var, out, new_mean, new_var,
-    cur, pre_n, pre_w, hid, spa, w_r, w_s, w_e, rows_all, stat_d, stat_r,
-    in_sem, out_sem, load_sem, w_send, w_recv, rows_send, rows_recv, d_send, d_recv, r_send, r_recv,
+    dp, rep, gather, slots_in, rates_in, images, w_reduce, w_spatial, w_expand, gains_in, offsets_in,
+    run_mean, run_var, pre_w, cur, factors, new_mean, new_var,
+    slot_ref, rate_ref, gammas, betas, pre_n, hid, spa, w_r, w_s, w_e, rows_all, stat_d, stat_r,
+    in_sem, load_sem, w_send, w_recv, rows_send, rows_recv, d_send, d_recv, r_send, r_recv,
 ):
     pix, wide_c = cur.shape
-    thin_c = pre_n.shape[2]
+    slabs = pre_n.shape[1]
+    thin_c = slabs * LANES
     imgs = pix // (SIDE * SIDE)
     half = imgs // 2
     count = 1.0 * pix * dp * rep
@@ -67,6 +69,12 @@
         copy.start()
     for copy in loads[1:]:
         copy.start()
+    small_loads = [
+        pltpu.make_async_copy(src, dst, load_sem.at[len(parts) + 2 + i])
+        for i, (src, dst) in enumerate(
+            [(slots_in, slot_ref), (rates_in, rate_ref), (gains_in, gammas), (offsets_in, betas)]
+        )
+    ]
     step = pix // 7
     image_loads = [
         pltpu.make_async_copy(
@@ -74,7 +82,7 @@
         )
         for i in range(7)
     ]
-    for copy in image_loads:
+    for copy in image_loads + small_loads:
         copy.start()
 
     barrier = pltpu.get_barrier_semaphore()
@@ -89,8 +97,8 @@
     hid[:, 0:1] = jnp.zeros((imgs, 1, WIDE, hid.shape[3]), hid.dtype)
     hid[:, SIDE + 1 : SIDE + 2] = jnp.zeros((imgs, 1, WIDE, hid.shape[3]), hid.dtype)
     duo = 2 * SIDE * SIDE
-    pre_n[:, 0:MARGIN] = jnp.zeros((imgs // 2, MARGIN, thin_c), jnp.float32)
-    pre_n[:, MARGIN + duo :] = jnp.zeros((imgs // 2, WIDE, thin_c), jnp.float32)
+    pre_n[:, :, 0:MARGIN] = jnp.zeros((imgs // 2, slabs, MARGIN, LANES), jnp.float32)
+    pre_n[:, :, MARGIN + duo :] = jnp.zeros((imgs // 2, slabs, WIDE, LANES), jnp.float32)
     pl.semaphore_wait(barrier, dp + rep - 2)
 
     pending = []
@@ -148,7 +156,7 @@
         pending.append(copy)
         row_copies.append(copy)
     w_begin(1)
-    for copy in image_loads:
+    for copy in image_loads + small_loads:
         copy.wait()
     w_forward(0)
     w_finish(0)
@@ -166,7 +174,7 @@
             copy.start()
             pending.append(copy)
 
-    def moments_end(layer, n):
+    def moments_end(layer, n, begins, forwards):
         for k in range(1, dp):
             ref = stat_d.at[layer, lax.rem(me + dp - k, dp), :, pl.ds(0, n)]
             remote(
@@ -181,6 +189,10 @@
             )
             copy.start()
             pending.append(copy)
+        for part in begins:
+            w_begin(part)
+        for part in forwards:
+            w_forward(part)
         for k in range(1, rep):
             ref = stat_r.at[layer, lax.rem(mine + rep - k, rep), :, pl.ds(0, n)]
             remote(
@@ -215,9 +227,9 @@
 
     chunk = half * SIDE * SIDE
 
-    def narrow(c):
-        value = pre_n[c * (half // 2) : (c + 1) * (half // 2), MARGIN : MARGIN + duo]
-        return value.reshape(chunk, thin_c)
+    def narrow(c, t):
+        value = pre_n[c * (half // 2) : (c + 1) * (half // 2), t, MARGIN : MARGIN + duo]
+        return value.reshape(chunk, LANES)
 
     scale3 = bias3 = None
     for b in range(BLOCKS):
@@ -230,36 +242,36 @@
                 ).astype(cur.dtype)
             pre = jnp.dot(cur[at], w_r[b], preferred_element_type=jnp.float32)
             for i in range(half // 2):
-                pre_n[c * (half // 2) + i, MARGIN : MARGIN + duo] = pre[i * duo : (i + 1) * duo]
+                for t in range(slabs):
+                    pre_n[c * (half // 2) + i, t, MARGIN : MARGIN + duo] = pre[
+                        i * duo : (i + 1) * duo, t * LANES : (t + 1) * LANES
+                    ]
             acc = add(acc, sums(pre))
         moments_begin(3 * b, *acc)
         if b == 0:
-            w_begin(2)
-            w_begin(3)
-            w_forward(1)
-            for k, copy in enumerate(row_copies):
+            for copy in row_copies:
                 copy.wait_recv()
-        else:
-            w_forward(5)
-        scale, bias = moments_end(3 * b, thin_c)
+        scale, bias = moments_end(3 * b, thin_c, *(((2, 3), (1,)) if b == 0 else ((), (5,))))
         w_finish(3 * b + 1)
 
-        column = lax.broadcasted_iota(jnp.int32, (WIDE, thin_c), 0)
+        column = lax.broadcasted_iota(jnp.int32, (WIDE, LANES), 0)
 
         def fill(pair, carry):
-            for i in range(2):
-                for r in range(SIDE):
-                    for dx in range(3):
-                        start = MARGIN + i * SIDE * SIDE + r * SIDE + dx - 1
-                        value = pre_n[pair, start : start + WIDE]
-                        value = jax.nn.relu(value * scale + bias)
-                        if dx == 0:
-                            value = jnp.where(column == 0, 0.0, value)
-                        if dx == 2:
-                            value = jnp.where(column == SIDE - 1, 0.0, value)
-                        hid[pair * 2 + i, r + 1, :, dx * thin_c : (dx + 1) * thin_c] = (
-                            value.astype(hid.dtype)
-                        )
+            for t in range(slabs):
+                lanes = slice(t * LANES, (t + 1) * LANES)
+                scale_t, bias_t = scale[:, lanes], bias[:, lanes]
+                for i in range(2):
+                    for r in range(SIDE):
+                        for dx in range(3):
+                            start = MARGIN + i * SIDE * SIDE + r * SIDE + dx - 1
+                            value = pre_n[pair, t, start : start + WIDE]
+                            value = jax.nn.relu(value * scale_t + bias_t)
+                            if dx == 0:
+                                value = jnp.where(column == 0, 0.0, value)
+                            if dx == 2:
+                                value = jnp.where(column == SIDE - 1, 0.0, value)
+                            at = dx * thin_c + t * LANES
+                            hid[pair * 2 + i, r + 1, :, at : at + LANES] = value.astype(hid.dtype)
             return carry
 
         lax.fori_loop(0, imgs // 2, fill, 0)
@@ -276,46 +288,51 @@
                 pre = term if pre is None else pre + term
             for r in range(half * SIDE):
                 pair, start = divmod(c * chunk + r * SIDE, duo)
-                pre_n[pair, MARGIN + start : MARGIN + start + SIDE] = pre[
-                    r * WIDE : r * WIDE + SIDE
-                ]
-            acc = add(acc, sums(narrow(c)))
+                for t in range(slabs):
+                    pre_n[pair, t, MARGIN + start : MARGIN + start + SIDE] = pre[
+                        r * WIDE : r * WIDE + SIDE, t * LANES : (t + 1) * LANES
+                    ]
+            here = [sums(narrow(c, t)) for t in range(slabs)]
+            acc = add(acc, tuple(jnp.concatenate(row, axis=1) for row in zip(*here)))
         moments_begin(3 * b + 1, *acc)
-        if b == 0:
-            w_begin(4)
-            w_forward(2)
-            w_forward(3)
-        scale, bias = moments_end(3 * b + 1, thin_c)
+        scale, bias = moments_end(3 * b + 1, thin_c, *(((4,), (2, 3)) if b == 0 else ((), ())))
         w_finish(3 * b + 2)
 
         acc = None
         for c in range(2):
             at = pl.ds(c * chunk, chunk)
-            spa[at] = jax.nn.relu(
-                narrow(c) * scale + bias
-            ).astype(spa.dtype)
+            for t in range(slabs):
+                lanes = slice(t * LANES, (t + 1) * LANES)
+                spa[at, lanes] = jax.nn.relu(
+                    narrow(c, t) * scale[:, lanes] + bias[:, lanes]
+                ).astype(spa.dtype)
             pre = jnp.dot(spa[at], w_e[b], preferred_element_type=jnp.float32)
             pre_w[at] = pre
             acc = add(acc, sums(pre))
         moments_begin(3 * b + 2, *acc)
-        if b == 0:
-            w_begin(5)
-            w_forward(4)
-        scale3, bias3 = moments_end(3 * b + 2, wide_c)
+        scale3, bias3 = moments_end(3 * b + 2, wide_c, *(((5,), (4,)) if b == 0 else ((), ())))
         if b == 0:
             w_finish(3)
 
+    factors[0:1] = scale3
+    factors[1:2] = bias3
+    for copy in pending:
+        copy.wait_send()
+
+
+def finish(pre_w, cur, factors, old_mean, old_var, out, new_mean, new_var, buf, out_sem):
+    new_mean[...] = old_mean[...]
+    new_var[...] = old_var[...]
+    step = cur.shape[0] // 7
     stores = []
     for i in range(7):
         at = pl.ds(i * step, step)
-        cur[at] = jax.nn.relu(
-            pre_w[at] * scale3 + bias3 + cur[at].astype(jnp.float32)
+        buf[at] = jax.nn.relu(
+            pre_w[at] * factors[0:1] + factors[1:2] + cur[at].astype(jnp.float32)
         ).astype(cur.dtype)
-        copy = pltpu.make_async_copy(cur.at[at], out.at[at], out_sem.at[i])
+        copy = pltpu.make_async_copy(buf.at[at], out.at[at], out_sem.at[i])
         copy.start()
         stores.append(copy)
-    for copy in pending:
-        copy.wait_send()
     for copy in stores:
         copy.wait()
 
@@ -336,26 +353,29 @@
         w_reduce, w_spatial, w_expand = [
             lax.all_gather(w, "dp", axis=1, tiled=True) for w in (w_reduce, w_spatial, w_expand)
         ]
-    anywhere = pl.BlockSpec(memory_space=pl.ANY)
+    anywhere = pl.BlockSpec(memory_space=pltpu.HBM)
     vmem = pl.BlockSpec(memory_space=pltpu.VMEM)
-    smem = pl.BlockSpec(memory_space=pltpu.SMEM)
     bf16, f32 = jnp.bfloat16, jnp.float32
     dma = pltpu.SemaphoreType.DMA
     parts = 3 * BLOCKS
-    return pl.pallas_call(
+    held = pl.pallas_call(
         functools.partial(kernel, dp, rep, gather),
         name="recalibrate",
         out_shape=(
+            jax.ShapeDtypeStruct(images.shape, f32),
             jax.ShapeDtypeStruct(images.shape, bf16),
+            jax.ShapeDtypeStruct((2, wide_c), f32),
             jax.ShapeDtypeStruct(run_mean.shape, f32),
             jax.ShapeDtypeStruct(run_var.shape, f32),
         ),
-        in_specs=[smem, smem] + [anywhere] * 4 + [vmem, vmem, anywhere, anywhere],
-        out_specs=(anywhere, vmem, vmem),
+        in_specs=[anywhere] * 10,
+        out_specs=(vmem,) * 5,
         scratch_shapes=[
-            pltpu.VMEM((pix, wide_c), bf16),
-            pltpu.VMEM((imgs // 2, MARGIN + 2 * SIDE * SIDE + WIDE, thin_c), f32),
-            pltpu.VMEM((pix, wide_c), f32),
+            pltpu.SMEM(slot_table.shape, jnp.int32),
+            pltpu.SMEM(momenta.shape, f32),
+            pltpu.VMEM(gammas.shape, f32),
+            pltpu.VMEM(betas.shape, f32),
+            pltpu.VMEM((imgs // 2, thin_c // LANES, MARGIN + 2 * SIDE * SIDE + WIDE, LANES), f32),
             pltpu.VMEM((imgs, SIDE + 2, WIDE, 3 * thin_c), bf16),
             pltpu.VMEM((pix, thin_c), bf16),
             pltpu.VMEM((BLOCKS, wide_c, thin_c), bf16),
@@ -365,8 +385,7 @@
             pltpu.VMEM((LAYERS, dp, 2, wide_c), f32),
             pltpu.VMEM((LAYERS, rep, 2, wide_c), f32),
             dma((7,)),
-            dma((7,)),
-            dma((parts + 2,)),
+            dma((parts + 6,)),
             dma((parts, dp)),
             dma((parts, dp)),
             dma((dp,)),
@@ -377,9 +396,30 @@
             dma((LAYERS, rep)),
         ],
         compiler_params=pltpu.CompilerParams(
-            collective_id=0, has_side_effects=True, vmem_limit_bytes=60 * 1024 * 1024
+            collective_id=0, has_side_effects=True, vmem_limit_bytes=40 * 1024 * 1024
         ),
-    )(slot_table, momenta, images, w_reduce, w_spatial, w_expand, gammas, betas, run_mean, run_var)
+    )(
+        *[
+            pltpu.with_memory_space_constraint(given, pltpu.HBM)
+            for given in (
+                slot_table, momenta, images, w_reduce, w_spatial, w_expand, gammas, betas,
+                run_mean, run_var,
+            )
+        ]
+    )
+    return pl.pallas_call(
+        finish,
+        name="finish",
+        out_shape=(
+            jax.ShapeDtypeStruct(images.shape, bf16),
+            jax.ShapeDtypeStruct(run_mean.shape, f32),
+            jax.ShapeDtypeStruct(run_var.shape, f32),
+        ),
+        in_specs=[vmem] * 5,
+        out_specs=(anywhere, vmem, vmem),
+        scratch_shapes=[pltpu.VMEM((pix, wide_c), bf16), dma((7,))],
+        compiler_params=pltpu.CompilerParams(vmem_limit_bytes=32 * 1024 * 1024),
+    )(*held)
 
 
 def solution(mesh):

time: 78.9 us -> 72.9 us (0.924)
  local copies, waits for them, and re-layouts: 5.1 us -> 0 us
  Pallas kernels: 72.9 us -> 72.1 us
    unnamed x7 -> x0, local copies, waits for them, and re-layouts: 5.1 us -> none
    pallas_call x1, Pallas kernels: 72.9 us -> 69.6 us  [body(): pl.pallas_call(functools.partial(kernel, dp, rep, gather), name='recalibr...]
    pallas_call x0 -> x1, Pallas kernels: none -> 2.57 us  [body(): pl.pallas_call(finish, name='finish', out_shape=(jax.ShapeDtypeStruct(ima...]
where the time goes in v2:
time: 72.9 us; the launch traced here: 72.8 us
  Pallas kernels  72.1 us (99%)
    pallas_call x1, Pallas kernels, body(): pl.pallas_call(functools.partial(kernel, dp, rep, gather), name='recalibr...  69.6 us
    pallas_call x1, Pallas kernels, body(): pl.pallas_call(finish, name='finish', out_shape=(jax.ShapeDtypeStruct(ima...  2.57 us

profile of v2, /device:TPU:0, one launch (start us, length us, event | category | flops | bytes accessed | tf_op | source)
XLA Modules:
  0.0 72.8 jit_solution(6527327331515877034)
XLA Ops:
  0.6 69.6 %recalibrate.1 = (f32[1568,1024]{1,0:T(8,128)S(1)}, bf16[1568,1024]{1,0:T(8,128)(2,1)S(1)}, f32[2,1024]{1,0:T(2,128)S(1)}, f32[1,1024]{1,0:T(1,128)S(1)}, f32[1,1024]{1,0:T(1,128)S(1)}) custom-call(s32[8]{0:T(128)} %slots_in.1, f32[6]{0:T(128)} %rates_in.1, bf16[1568,1024]{1,0:T(8,128)(2,1)} %images.1, bf16[2,128,256]{2,1,0:T(8,128)(2,1)} %w_reduce.1, ...), custom_call_target="tpu_custom_call" | custom-call | tf_op jit(solution)/shard_map/recalibrate/pallas_call | solution.py:361
  70.2 2.6 %finish.1 = (bf16[1568,1024]{1,0:T(8,128)(2,1)}, f32[1,1024]{1,0:T(1,128)}, f32[1,1024]{1,0:T(1,128)}) custom-call(f32[1568,1024]{1,0:T(8,128)S(1)} %get-tuple-element.8.pre_w, bf16[1568,1024]{1,0:T(8,128)(2,1)S(1)} %get-tuple-element.9.cur, f32[2,1024]{1,0:T(2,128)S(1)} %get-tuple-element.10.factors, f32[1,1024]{1,0:T(1,128)S(1)} %get-tuple-element.11.old_mean, ...), custom_call_target="tpu_custom_call" | custom-call | tf_op jit(solution)/shard_map/finish/pallas_call | solution.py:410

commit v3 on v2

--- a/solution.py
+++ b/solution.py
@@ -251,7 +251,7 @@
         if b == 0:
             for copy in row_copies:
                 copy.wait_recv()
-        scale, bias = moments_end(3 * b, thin_c, *(((2, 3), (1,)) if b == 0 else ((), (5,))))
+        scale, bias = moments_end(3 * b, thin_c, *(((2,), (1,)) if b == 0 else ((5,), (4,))))
         w_finish(3 * b + 1)
 
         column = lax.broadcasted_iota(jnp.int32, (WIDE, LANES), 0)
@@ -274,9 +274,10 @@
                             hid[pair * 2 + i, r + 1, :, at : at + LANES] = value.astype(hid.dtype)
             return carry
 
-        lax.fori_loop(0, imgs // 2, fill, 0)
         acc = None
         for c in range(2):
+            for pair in range(c * (half // 2), (c + 1) * (half // 2)):
+                fill(pair, 0)
             pre = None
             for dy in range(3):
                 lhs = hid[c * half : (c + 1) * half, dy : dy + SIDE]
@@ -295,7 +296,7 @@
             here = [sums(narrow(c, t)) for t in range(slabs)]
             acc = add(acc, tuple(jnp.concatenate(row, axis=1) for row in zip(*here)))
         moments_begin(3 * b + 1, *acc)
-        scale, bias = moments_end(3 * b + 1, thin_c, *(((4,), (2, 3)) if b == 0 else ((), ())))
+        scale, bias = moments_end(3 * b + 1, thin_c, *(((3,), (2,)) if b == 0 else ((), (5,))))
         w_finish(3 * b + 2)
 
         acc = None
@@ -310,7 +311,7 @@
             pre_w[at] = pre
             acc = add(acc, sums(pre))
         moments_begin(3 * b + 2, *acc)
-        scale3, bias3 = moments_end(3 * b + 2, wide_c, *(((5,), (4,)) if b == 0 else ((), ())))
+        scale3, bias3 = moments_end(3 * b + 2, wide_c, *(((4,), (3,)) if b == 0 else ((), ())))
         if b == 0:
             w_finish(3)
 

time: 72.9 us -> 71.3 us (0.978)
  Pallas kernels: 72.1 us -> 70.5 us
    pallas_call x1, Pallas kernels: 69.6 us -> 68 us  [body(): pl.pallas_call(functools.partial(kernel, dp, rep, gather), name='recalibr...]
where the time goes in v3:
time: 71.3 us; the launch traced here: 71.2 us
  Pallas kernels  70.5 us (99%)
    pallas_call x1, Pallas kernels, body(): pl.pallas_call(functools.partial(kernel, dp, rep, gather), name='recalibr...  68 us
    pallas_call x1, Pallas kernels, body(): pl.pallas_call(finish, name='finish', out_shape=(jax.ShapeDtypeStruct(ima...  2.57 us

profile of v3, /device:TPU:0, one launch (start us, length us, event | category | flops | bytes accessed | tf_op | source)
XLA Modules:
  0.0 71.2 jit_solution(16844346749602792643)
XLA Ops:
  0.6 68.0 %recalibrate.1 = (f32[1568,1024]{1,0:T(8,128)S(1)}, bf16[1568,1024]{1,0:T(8,128)(2,1)S(1)}, f32[2,1024]{1,0:T(2,128)S(1)}, f32[1,1024]{1,0:T(1,128)S(1)}, f32[1,1024]{1,0:T(1,128)S(1)}) custom-call(s32[8]{0:T(128)} %slots_in.1, f32[6]{0:T(128)} %rates_in.1, bf16[1568,1024]{1,0:T(8,128)(2,1)} %images.1, bf16[2,128,256]{2,1,0:T(8,128)(2,1)} %w_reduce.1, ...), custom_call_target="tpu_custom_call" | custom-call | tf_op jit(solution)/shard_map/recalibrate/pallas_call | solution.py:362
  68.6 2.6 %finish.1 = (bf16[1568,1024]{1,0:T(8,128)(2,1)}, f32[1,1024]{1,0:T(1,128)}, f32[1,1024]{1,0:T(1,128)}) custom-call(f32[1568,1024]{1,0:T(8,128)S(1)} %get-tuple-element.8.pre_w, bf16[1568,1024]{1,0:T(8,128)(2,1)S(1)} %get-tuple-element.9.cur, f32[2,1024]{1,0:T(2,128)S(1)} %get-tuple-element.10.factors, f32[1,1024]{1,0:T(1,128)S(1)} %get-tuple-element.11.old_mean, ...), custom_call_target="tpu_custom_call" | custom-call | tf_op jit(solution)/shard_map/finish/pallas_call | solution.py:411
